TPU v7x, 32 devices: a whole 2x2x4 slice. The times are simulated.
32 devices in a mesh: cells: 16 (over z, y, x), faces: 2 (over core).
Axes of the slice: x: 2, y: 2, z: 4, core: 2. Of those that a mesh axis runs over, the one named last changes fastest.
Arguments:
- flow_state: float32 [4, 131072], P(None, 'cells'), may hold values from -6 to 6
- source_term: float32 [4, 131072], P(None, 'cells'), may hold values from -24 to 24
- volume_rate: float32 [131072], P('cells'), may hold values from 0.5 to 4
- face_normal: float32 [3, 393216], P(None, ('cells', 'faces')), may hold values from -3 to 3
- face_owner: int32 [393216], P(('cells', 'faces')), may hold values from 0 to 8191, as said below
- face_neighbour: int32 [393216], P(('cells', 'faces')), may hold values from 0 to 9727, as said below
- face_count: int32 [32], P(('cells', 'faces')), may hold values from 1536 to 12288, as said below
- send_list: int32 [96, 256], P('cells'), may hold values from 0 to 8191
- halo_count: int32 [96], P('cells'), may hold values from 64 to 256, as said below
Outputs:
- solution_field: float32 [4, 131072], P(None, 'cells')
- residual: float32 [4, 131072], P(None, 'cells')
Inputs may be any that keep to these rules, and one draw needn't show every extreme that they name: `face_owner`: A local cell of the slot's partition; with s = g mod 12288 and t = s // 192, it lies in 128 * t to 128 * t + 127. `face_neighbour`: with s and t as for face_owner: below 8192 a local cell (128 * t + d) mod 8192 with d in 0 to 255; otherwise 8192 plus a halo slot of the slot's partition in (t mod (6)) * 256 to that plus 256 - 1. Live slots of a block are its first face_count slots; in every draw some block has all 12288 slots live. `send_list`: entries at or past the list's count are unused. `halo_count`: every partition has one list with exactly 256 entries.
All inputs are finite; a program needn't handle non-finite values.
Results may differ from a plain program's by a relative error of at most 0.0003.
Values sent between devices are 32-bit elements; how exact they have to be, the bound alone decides.
No kernel may reach another device: no remote copies, remote signals or barrier semaphores. Data moves between devices by JAX's collectives and lax.ppermute only.
A program may use at most 64 MiB of HBM per device.

v0:
```python
import jax
import jax.numpy as jnp
import numpy as np
from jax import lax
from jax.sharding import PartitionSpec as P

ITERS = 2


def passed_along(block, axis, distance):
    devices = range(lax.axis_size(axis))
    route = [((i - distance) % len(devices), i) for i in devices]
    return lax.ppermute(block, axis, route)


def offsets(count):
    return [which + 1 for which in range(count)] + [-(which + 1) for which in range(count)]


def body(
    flow_state,
    source_term,
    volume_rate,
    face_normal,
    face_owner,
    face_neighbour,
    face_count,
    send_list,
    halo_count,
):
    highest = lax.Precision.HIGHEST
    cells_here = flow_state.shape[1]
    list_total, slot_width = send_list.shape
    shift_list = offsets(list_total // 2)
    slot_ids = lax.broadcasted_iota(jnp.int32, (list_total, slot_width), 1)
    keep_mask = (slot_ids < halo_count[:, None]).astype(jnp.float32)
    tiles = cells_here // 128
    slot_total = face_owner.shape[0]
    per_tile = slot_total // tiles
    halo_total = list_total * slot_width
    window = max(slot_width, halo_total // tiles)
    window_count = halo_total // window
    window_pick = np.arange(tiles) % window_count
    tile_ids = lax.broadcasted_iota(jnp.int32, (tiles, per_tile), 0)
    owner_tiled = face_owner.reshape(tiles, per_tile)
    neighbour_tiled = face_neighbour.reshape(tiles, per_tile)
    is_local_tiled = neighbour_tiled < cells_here
    owner_column = owner_tiled - tile_ids * 128
    local_column = jnp.where(is_local_tiled, (neighbour_tiled - tile_ids * 128) % cells_here, -1)
    halo_column = jnp.where(
        is_local_tiled, -1, neighbour_tiled - cells_here - tile_ids % window_count * window
    )
    owner_hot = (
        owner_column[:, :, None] == lax.broadcasted_iota(jnp.int32, (1, 1, 128), 2)
    ).astype(jnp.float32)
    local_hot = (
        local_column[:, :, None] == lax.broadcasted_iota(jnp.int32, (1, 1, 256), 2)
    ).astype(jnp.float32)
    halo_hot = (
        halo_column[:, :, None] == lax.broadcasted_iota(jnp.int32, (1, 1, window), 2)
    ).astype(jnp.float32)
    is_live = (
        lax.broadcasted_iota(jnp.int32, (tiles, per_tile), 0) * per_tile
        + lax.broadcasted_iota(jnp.int32, (tiles, per_tile), 1)
        < face_count[0]
    ).astype(jnp.float32)
    local_weight = is_local_tiled.astype(jnp.float32)
    normal_tiled = face_normal.reshape(3, tiles, per_tile)

    def ghosts(vector_in):
        outgoing = (
            jnp.stack(
                [jnp.take(vector_in, send_list[which], axis=1) for which in range(list_total)]
            )
            * keep_mask[:, None, :]
        )
        incoming = jnp.stack(
            [
                passed_along(outgoing[which], "cells", shift_list[which])
                for which in range(list_total)
            ]
        )
        return jnp.transpose(incoming, (1, 0, 2)).reshape(vector_in.shape[0], halo_total)

    def to_faces(vector_in):
        rows = vector_in.shape[0]
        blocks = vector_in.reshape(rows, tiles, 128)
        paired = jnp.concatenate([blocks, jnp.roll(blocks, -1, axis=1)], axis=2)
        halo_cells = ghosts(vector_in)
        halo_windows = halo_cells.reshape(rows, window_count, window)[:, window_pick]
        left_side = jnp.einsum("tfc,btc->btf", owner_hot, blocks, precision=highest)
        right_side = jnp.einsum("tfc,btc->btf", local_hot, paired, precision=highest)
        right_side = right_side + jnp.einsum(
            "tfc,btc->btf", halo_hot, halo_windows, precision=highest
        )
        return (left_side, right_side)

    def to_cells(owner_values, neighbour_values):
        rows = owner_values.shape[0]
        owned = jnp.einsum("tfc,btf->btc", owner_hot, owner_values, precision=highest)
        beside = jnp.einsum("tfc,btf->btc", local_hot, neighbour_values, precision=highest)
        summed = owned + beside[:, :, :128] + jnp.roll(beside[:, :, 128:], 1, axis=1)
        return summed.reshape(rows, cells_here)

    left_state, right_state = to_faces(flow_state)
    normal_speed = 0.5 * jnp.sum(normal_tiled * (left_state[:3] + right_state[:3]), axis=0)
    normal_size = jnp.sqrt(jnp.sum(normal_tiled * normal_tiled, axis=0))
    wave_speed = jnp.abs(normal_speed) + 2.0 * normal_size
    owner_terms = (
        0.5
        * jnp.concatenate([normal_speed[None], normal_tiled, wave_speed[None]], axis=0)
        * is_live
    )
    neighbour_terms = jnp.concatenate(
        [-0.5 * normal_speed[None], -0.5 * normal_tiled, 0.5 * wave_speed[None]], axis=0
    ) * (is_live * local_weight)
    block_terms = lax.psum(to_cells(owner_terms, neighbour_terms), "faces")
    velocity_diag = volume_rate + block_terms[0] + block_terms[4]
    pressure_diag = volume_rate + block_terms[4]
    coupling = block_terms[1:4]
    schur = pressure_diag - jnp.sum(coupling * coupling, axis=0) / velocity_diag

    def precondition(vector_in):
        pressure = (
            vector_in[3] - jnp.sum(coupling * vector_in[:3], axis=0) / velocity_diag
        ) / schur
        velocity = (vector_in[:3] - coupling * pressure) / velocity_diag
        return jnp.concatenate([velocity, pressure[None]], axis=0)

    def apply_matrix(vector_in):
        left_side, right_side = to_faces(vector_in)
        face_sum = left_side + right_side
        central = jnp.concatenate(
            [
                normal_speed * face_sum[:3] + normal_tiled * face_sum[3],
                jnp.sum(normal_tiled * face_sum[:3], axis=0)[None],
            ],
            axis=0,
        )
        face_flux = (0.5 * central - 0.5 * wave_speed * (right_side - left_side)) * is_live
        partial_value = to_cells(face_flux, -face_flux * local_weight)
        return volume_rate * vector_in + lax.psum(partial_value, "faces")

    solution_field = jnp.zeros_like(source_term)
    residual = source_term
    direction = source_term
    rho_now = lax.psum(jnp.sum(source_term * residual), "cells")
    for iteration in range(ITERS):
        pre_dir = precondition(direction)
        image = apply_matrix(pre_dir)
        step_alpha = rho_now / lax.psum(jnp.sum(source_term * image), "cells")
        middle = residual - step_alpha * image
        pre_mid = precondition(middle)
        second = apply_matrix(pre_mid)
        second_mid, second_sq, shadow_mid, shadow_second = lax.psum(
            (
                jnp.sum(second * middle),
                jnp.sum(second * second),
                jnp.sum(source_term * middle),
                jnp.sum(source_term * second),
            ),
            "cells",
        )
        step_omega = second_mid / second_sq
        solution_field = solution_field + step_alpha * pre_dir + step_omega * pre_mid
        residual = middle - step_omega * second
        rho_next = shadow_mid - step_omega * shadow_second
        if iteration + 1 < ITERS:
            ratio_beta = rho_next / rho_now * (step_alpha / step_omega)
            direction = residual + ratio_beta * (direction - step_omega * image)
            rho_now = rho_next
    return (solution_field, residual)


def solution(mesh):
    in_specs = (
        P(None, "cells"),
        P(None, "cells"),
        P("cells"),
        P(None, ("cells", "faces")),
        P(("cells", "faces")),
        P(("cells", "faces")),
        P(("cells", "faces")),
        P("cells", None),
        P("cells"),
    )
    out_specs = (P(None, "cells"), P(None, "cells"))
    return jax.shard_map(body, mesh=mesh, in_specs=in_specs, out_specs=out_specs, check_vma=False)
```

profile of v0, /device:TPU:0, one launch (start us, length us, event | category | flops | bytes accessed | tf_op | source)
XLA Modules:
  0.0 638.8 jit_solution(4085861947890233693)
XLA Ops:
  42.0 6.4 fusion.61
  54.7 6.8 %fusion.4 = f32[64,4,192]{2,1,0:T(4,128)S(1)} fusion(s32[64,192]{1,0:T(8,128)S(1)} %get-tuple-element.48, f32[64,4,256]{2,1,0:T(4,128)S(1)} %gather_fusion), kind=kOutput, calls=%fused_computation.40 | convolution fusion | flops 154140672 | bytes 507904 | tf_op jit(solution)/shard_map/tfc,btc->btf/dot_general | solution.py:93
  61.5 6.9 %fusion.56 = f32[4,64,192]{2,0,1:T(4,128)S(1)} fusion(f32[64,4,192]{2,1,0:T(4,128)S(1)} %fusion.4, s32[64,192]{1,0:T(8,128)S(1)} %get-tuple-element.47, f32[4,1,128]{2,0,1:T(4,128)S(1)} %slice.454, f32[4,63,128]{2,0,1:T(4,128)S(1)} %slice.453, f32[4,64,128]{2,0,1:T(4,128)S(1)} %bitcast.444), kind=kOutput, calls=%fused_computation.94 | convolution fusion | flops 154320896 | bytes 704512 | tf_op jit(solution)/shard_map/tfc,btc->btf/dot_general | solution.py:92
  68.8 6.9 %fusion.50 = f32[5,64,256]{2,0,1:T(8,128)S(1)} fusion(s32[64,192]{1,0:T(8,128)S(1)} %get-tuple-element.47, f32[5,64,192]{2,1,0:T(8,128)S(1)} %maximum_multiply_fusion.1), kind=kOutput, calls=%fused_computation.88 | convolution fusion | flops 191889408 | bytes 622592 | tf_op jit(solution)/shard_map/tfc,btf->btc/dot_general | solution.py:101
  81.3 18.1 %all-reduce.9.cloned.1.call-done = f32[5,8192]{1,0:T(8,128)} async-done(((f32[5,8192]{1,0:T(8,128)}), f32[5,8192]{1,0:T(8,128)}) %all-reduce.9.cloned.1.call-update) | async-done | bytes 163856 | tf_op jit(solution)/shard_map/psum | solution.py:117
  123.0 6.4 fusion.37
  145.3 6.8 %fusion.3 = f32[64,4,192]{2,1,0:T(4,128)S(1)} fusion(s32[64,192]{1,0:T(8,128)S(1)} %get-tuple-element.48, f32[64,4,256]{2,1,0:T(4,128)S(1)} %gather_fusion.1), kind=kOutput, calls=%fused_computation.39 | convolution fusion | flops 154140672 | bytes 507904 | tf_op jit(solution)/shard_map/tfc,btc->btf/dot_general | solution.py:93
  152.1 6.9 %fusion.57 = f32[64,4,192]{2,1,0:T(4,128)S(1)} fusion(f32[64,4,192]{2,1,0:T(4,128)S(1)} %fusion.3, s32[64,192]{1,0:T(8,128)S(1)} %get-tuple-element.47, f32[4,1,128]{2,0,1:T(4,128)S(1)} %fusion.167, f32[4,63,128]{2,0,1:T(4,128)S(1)} %fusion.154, f32[1,64,128]{2,0,1:T(1,128)S(1)} %bitcast.425, f32[3,64,128]{2,0,1:T(4,128)S(1)} %bitcast.399), kind=kOutput, calls=%fused_computation.95 | convolution fusion | flops 154386432 | bytes 704512 | tf_op jit(solution)/shard_map/tfc,btc->btf/dot_general | solution.py:92
  170.6 17.9 %all-reduce.11.cloned.1.call-done = f32[4,8192]{1,0:T(4,128)} async-done(((f32[4,8192]{1,0:T(4,128)}), f32[4,8192]{1,0:T(4,128)}) %all-reduce.11.cloned.1.call-update) | async-done | bytes 131088 | tf_op jit(solution)/shard_map/psum | solution.py:142
  190.2 42.6 %all-reduce.2 = (f32[]{:T(128)}, f32[]{:T(128)}) all-reduce(f32[]{:T(128)} %get-tuple-element.16, f32[]{:T(128)} %get-tuple-element.15), channel_id=1, replica_groups=mesh['cells'=16,'faces'=2] {'cells'}, use_global_device_ids=true, to_apply=%region_1.2 | all-reduce | flops 2 | bytes 16 | tf_op jit(solution)/shard_map/psum | solution.py:147
  254.6 6.4 fusion.35
  275.2 6.8 %fusion.2 = f32[64,4,192]{2,1,0:T(4,128)S(1)} fusion(s32[64,192]{1,0:T(8,128)S(1)} %get-tuple-element.48, f32[64,4,256]{2,1,0:T(4,128)S(1)} %gather_fusion.2), kind=kOutput, calls=%fused_computation.38 | convolution fusion | flops 154140672 | bytes 507904 | tf_op jit(solution)/shard_map/tfc,btc->btf/dot_general | solution.py:93
  282.0 6.9 %fusion.58 = f32[64,4,192]{2,1,0:T(4,128)S(1)} fusion(f32[64,4,192]{2,1,0:T(4,128)S(1)} %fusion.2, s32[64,192]{1,0:T(8,128)S(1)} %get-tuple-element.47, f32[4,1,128]{2,0,1:T(4,128)S(1)} %fusion.166, f32[4,63,128]{2,0,1:T(4,128)S(1)} %fusion.153, f32[1,64,128]{2,0,1:T(1,128)S(1)} %bitcast.432, f32[3,64,128]{2,0,1:T(4,128)S(1)} %bitcast.403), kind=kOutput, calls=%fused_computation.96 | convolution fusion | flops 154386432 | bytes 704512 | tf_op jit(solution)/shard_map/tfc,btc->btf/dot_general | solution.py:92
  300.4 18.5 %all-reduce.13.cloned.1.call-done = f32[4,8192]{1,0:T(4,128)} async-done(((f32[4,8192]{1,0:T(4,128)}), f32[4,8192]{1,0:T(4,128)}) %all-reduce.13.cloned.1.call-update) | async-done | bytes 131088 | tf_op jit(solution)/shard_map/psum | solution.py:142
  320.7 42.9 %all-reduce.1 = (f32[]{:T(128)}, f32[]{:T(128)}, f32[]{:T(128)}, f32[]{:T(128)}) all-reduce(f32[]{:T(128)} %get-tuple-element.14, f32[]{:T(128)} %get-tuple-element.13, f32[]{:T(128)} %get-tuple-element.12, f32[]{:T(128)} %get-tuple-element.11), channel_id=1, replica_groups=mesh['cells'=16,'faces'=2] {'cells'}, use_global_device_ids=true, to_apply=%region_19.21 | all-reduce | flops 4 | bytes 32 | tf_op jit(solution)/shard_map/psum | solution.py:155
  389.9 6.4 fusion.33
  410.5 6.8 %fusion.1 = f32[64,4,192]{2,1,0:T(4,128)S(1)} fusion(s32[64,192]{1,0:T(8,128)S(1)} %get-tuple-element.48, f32[64,4,256]{2,1,0:T(4,128)S(1)} %gather_fusion.3), kind=kOutput, calls=%fused_computation.37 | convolution fusion | flops 154140672 | bytes 507904 | tf_op jit(solution)/shard_map/tfc,btc->btf/dot_general | solution.py:93
  417.3 6.9 %fusion.59 = f32[64,4,192]{2,1,0:T(4,128)S(1)} fusion(f32[64,4,192]{2,1,0:T(4,128)S(1)} %fusion.1, s32[64,192]{1,0:T(8,128)S(1)} %get-tuple-element.47, f32[4,1,128]{2,0,1:T(4,128)S(1)} %fusion.165, f32[4,63,128]{2,0,1:T(4,128)S(1)} %fusion.152, f32[1,64,128]{2,0,1:T(1,128)S(1)} %bitcast.417, f32[3,64,128]{2,0,1:T(4,128)S(1)} %bitcast.395), kind=kOutput, calls=%fused_computation.97 | convolution fusion | flops 154386432 | bytes 704512 | tf_op jit(solution)/shard_map/tfc,btc->btf/dot_general | solution.py:92
  435.8 18.5 %all-reduce.15.cloned.1.call-done = f32[4,8192]{1,0:T(4,128)} async-done(((f32[4,8192]{1,0:T(4,128)}), f32[4,8192]{1,0:T(4,128)}) %all-reduce.15.cloned.1.call-update) | async-done | bytes 131088 | tf_op jit(solution)/shard_map/psum | solution.py:142
  455.9 42.6 %psum.108 = f32[]{:T(128)} all-reduce(f32[]{:T(128)} %multiply_reduce_fusion.4), channel_id=1, replica_groups=mesh['cells'=16,'faces'=2] {'cells'}, use_global_device_ids=true, to_apply=%region_26.28 | all-reduce | flops 1 | bytes 8 | tf_op jit(solution)/shard_map/psum | solution.py:151
  541.3 6.8 %fusion = f32[64,4,192]{2,1,0:T(4,128)S(1)} fusion(s32[64,192]{1,0:T(8,128)S(1)} %get-tuple-element.48, f32[64,4,256]{2,1,0:T(4,128)S(1)} %gather_fusion.4), kind=kOutput, calls=%fused_computation.36 | convolution fusion | flops 154140672 | bytes 507904 | tf_op jit(solution)/shard_map/tfc,btc->btf/dot_general | solution.py:93
  548.1 6.9 %fusion.60 = f32[64,4,192]{2,1,0:T(4,128)S(1)} fusion(f32[64,4,192]{2,1,0:T(4,128)S(1)} %fusion, s32[64,192]{1,0:T(8,128)S(1)} %get-tuple-element.47, f32[4,1,128]{2,0,1:T(4,128)S(1)} %fusion.164, f32[4,63,128]{2,0,1:T(4,128)S(1)} %fusion.151, f32[1,64,128]{2,0,1:T(1,128)S(1)} %bitcast.439, f32[3,64,128]{2,0,1:T(4,128)S(1)} %bitcast.407), kind=kOutput, calls=%fused_computation.98 | convolution fusion | flops 154386432 | bytes 704512 | tf_op jit(solution)/shard_map/tfc,btc->btf/dot_general | solution.py:92
  566.5 18.6 %all-reduce.17.cloned.1.call-done = f32[4,8192]{1,0:T(4,128)} async-done(((f32[4,8192]{1,0:T(4,128)}), f32[4,8192]{1,0:T(4,128)}) %all-reduce.17.cloned.1.call-update) | async-done | bytes 131088 | tf_op jit(solution)/shard_map/psum | solution.py:142
  586.7 42.6 %all-reduce = (f32[]{:T(128)}, f32[]{:T(128)}) all-reduce(f32[]{:T(128)} %get-tuple-element.10, f32[]{:T(128)} %get-tuple-element.9), channel_id=1, replica_groups=mesh['cells'=16,'faces'=2] {'cells'}, use_global_device_ids=true, to_apply=%region_31.33 | all-reduce | flops 2 | bytes 16 | tf_op jit(solution)/shard_map/psum | solution.py:155
  (381 shorter events, 250.8 us)
Async XLA Ops:
  7.2 92.2 %all-reduce.9.cloned.1.call-start = ((), (), s32[]{:S(2)}) async-start(), calls=%async_computation | async-start | bytes 524288 | tf_op jit(solution)/shard_map/psum | solution.py:117
  30.6 18.8 %collective-permute-start = (f32[4,256]{1,0:T(4,128)S(1)}, f32[4,256]{1,0:T(4,128)S(1)}, u32[]{:S(2)}, u32[]{:S(2)}) collective-permute-start(f32[4,256]{1,0:T(4,128)S(1)} %get-tuple-element.78), channel_id=1, source_target_pairs={{30,0},{0,2},{2,4},{4,6},{6,8},{8,10},{10,12},{12,14},{14,16},{16,... | collective-permute-start | bytes 12296 | tf_op jit(solution)/shard_map/ppermute | solution.py:13
  33.7 17.1 %collective-permute-start.1 = (f32[4,256]{1,0:T(4,128)S(1)}, f32[4,256]{1,0:T(4,128)S(1)}, u32[]{:S(2)}, u32[]{:S(2)}) collective-permute-start(f32[4,256]{1,0:T(4,128)S(1)} %get-tuple-element.77), channel_id=1, source_target_pairs={{28,0},{30,2},{0,4},{2,6},{4,8},{6,10},{8,12},{10,14},{12,16},{14,... | collective-permute-start | bytes 12296 | tf_op jit(solution)/shard_map/ppermute | solution.py:13
  35.2 15.6 %collective-permute-start.2 = (f32[4,256]{1,0:T(4,128)S(1)}, f32[4,256]{1,0:T(4,128)S(1)}, u32[]{:S(2)}, u32[]{:S(2)}) collective-permute-start(f32[4,256]{1,0:T(4,128)S(1)} %get-tuple-element.76), channel_id=1, source_target_pairs={{26,0},{28,2},{30,4},{0,6},{2,8},{4,10},{6,12},{8,14},{10,16},{12,... | collective-permute-start | bytes 12296 | tf_op jit(solution)/shard_map/ppermute | solution.py:13
  37.6 13.2 %collective-permute-start.3 = (f32[4,256]{1,0:T(4,128)S(1)}, f32[4,256]{1,0:T(4,128)S(1)}, u32[]{:S(2)}, u32[]{:S(2)}) collective-permute-start(f32[4,256]{1,0:T(4,128)S(1)} %get-tuple-element.75), channel_id=1, source_target_pairs={{2,0},{4,2},{6,4},{8,6},{10,8},{12,10},{14,12},{16,14},{18,16},{20... | collective-permute-start | bytes 12296 | tf_op jit(solution)/shard_map/ppermute | solution.py:13
  40.9 10.0 %collective-permute-start.4 = (f32[4,256]{1,0:T(4,128)S(1)}, f32[4,256]{1,0:T(4,128)S(1)}, u32[]{:S(2)}, u32[]{:S(2)}) collective-permute-start(f32[4,256]{1,0:T(4,128)S(1)} %get-tuple-element.74), channel_id=1, source_target_pairs={{4,0},{6,2},{8,4},{10,6},{12,8},{14,10},{16,12},{18,14},{20,16},{2... | collective-permute-start | bytes 12296 | tf_op jit(solution)/shard_map/ppermute | solution.py:13
  81.2 107.3 %all-reduce.11.cloned.1.call-start = ((), (), s32[]{:S(2)}) async-start(), calls=%async_computation.1 | async-start | bytes 262144 | tf_op jit(solution)/shard_map/psum | solution.py:142
  130.6 9.5 %collective-permute-start.6 = (f32[4,256]{1,0:T(4,128)S(1)}, f32[4,256]{1,0:T(4,128)S(1)}, u32[]{:S(2)}, u32[]{:S(2)}) collective-permute-start(f32[4,256]{1,0:T(4,128)S(1)} %get-tuple-element.72), channel_id=1, source_target_pairs={{30,0},{0,2},{2,4},{4,6},{6,8},{8,10},{10,12},{12,14},{14,16},{16,... | collective-permute-start | bytes 12296 | tf_op jit(solution)/shard_map/ppermute | solution.py:13
  132.4 8.8 %collective-permute-start.7 = (f32[4,256]{1,0:T(4,128)S(1)}, f32[4,256]{1,0:T(4,128)S(1)}, u32[]{:S(2)}, u32[]{:S(2)}) collective-permute-start(f32[4,256]{1,0:T(4,128)S(1)} %get-tuple-element.71), channel_id=1, source_target_pairs={{28,0},{30,2},{0,4},{2,6},{4,8},{6,10},{8,12},{10,14},{12,16},{14,... | collective-permute-start | bytes 12296 | tf_op jit(solution)/shard_map/ppermute | solution.py:13
  170.5 148.4 %all-reduce.13.cloned.1.call-start = ((), (), s32[]{:S(2)}) async-start(), calls=%async_computation.2 | async-start | bytes 262144 | tf_op jit(solution)/shard_map/psum | solution.py:142
  262.2 7.7 %collective-permute-start.12 = (f32[4,256]{1,0:T(4,128)S(1)}, f32[4,256]{1,0:T(4,128)S(1)}, u32[]{:S(2)}, u32[]{:S(2)}) collective-permute-start(f32[4,256]{1,0:T(4,128)S(1)} %get-tuple-element.66), channel_id=1, source_target_pairs={{30,0},{0,2},{2,4},{4,6},{6,8},{8,10},{10,12},{12,14},{14,16},{16,... | collective-permute-start | bytes 12296 | tf_op jit(solution)/shard_map/ppermute | solution.py:13
  262.3 10.6 %collective-permute-start.13 = (f32[4,256]{1,0:T(4,128)S(1)}, f32[4,256]{1,0:T(4,128)S(1)}, u32[]{:S(2)}, u32[]{:S(2)}) collective-permute-start(f32[4,256]{1,0:T(4,128)S(1)} %get-tuple-element.65), channel_id=1, source_target_pairs={{28,0},{30,2},{0,4},{2,6},{4,8},{6,10},{8,12},{10,14},{12,16},{14,... | collective-permute-start | bytes 12296 | tf_op jit(solution)/shard_map/ppermute | solution.py:13
  262.4 10.5 %collective-permute-start.14 = (f32[4,256]{1,0:T(4,128)S(1)}, f32[4,256]{1,0:T(4,128)S(1)}, u32[]{:S(2)}, u32[]{:S(2)}) collective-permute-start(f32[4,256]{1,0:T(4,128)S(1)} %get-tuple-element.64), channel_id=1, source_target_pairs={{26,0},{28,2},{30,4},{0,6},{2,8},{4,10},{6,12},{8,14},{10,16},{12,... | collective-permute-start | bytes 12296 | tf_op jit(solution)/shard_map/ppermute | solution.py:13
  262.4 10.5 %collective-permute-start.15 = (f32[4,256]{1,0:T(4,128)S(1)}, f32[4,256]{1,0:T(4,128)S(1)}, u32[]{:S(2)}, u32[]{:S(2)}) collective-permute-start(f32[4,256]{1,0:T(4,128)S(1)} %get-tuple-element.63), channel_id=1, source_target_pairs={{2,0},{4,2},{6,4},{8,6},{10,8},{12,10},{14,12},{16,14},{18,16},{20... | collective-permute-start | bytes 12296 | tf_op jit(solution)/shard_map/ppermute | solution.py:13
  300.4 153.9 %all-reduce.15.cloned.1.call-start = ((), (), s32[]{:S(2)}) async-start(), calls=%async_computation.3 | async-start | bytes 262144 | tf_op jit(solution)/shard_map/psum | solution.py:142
  397.5 7.7 %collective-permute-start.18 = (f32[4,256]{1,0:T(4,128)S(1)}, f32[4,256]{1,0:T(4,128)S(1)}, u32[]{:S(2)}, u32[]{:S(2)}) collective-permute-start(f32[4,256]{1,0:T(4,128)S(1)} %get-tuple-element.60), channel_id=1, source_target_pairs={{30,0},{0,2},{2,4},{4,6},{6,8},{8,10},{10,12},{12,14},{14,16},{16,... | collective-permute-start | bytes 12296 | tf_op jit(solution)/shard_map/ppermute | solution.py:13
  397.6 10.6 %collective-permute-start.19 = (f32[4,256]{1,0:T(4,128)S(1)}, f32[4,256]{1,0:T(4,128)S(1)}, u32[]{:S(2)}, u32[]{:S(2)}) collective-permute-start(f32[4,256]{1,0:T(4,128)S(1)} %get-tuple-element.59), channel_id=1, source_target_pairs={{28,0},{30,2},{0,4},{2,6},{4,8},{6,10},{8,12},{10,14},{12,16},{14,... | collective-permute-start | bytes 12296 | tf_op jit(solution)/shard_map/ppermute | solution.py:13
  397.7 10.5 %collective-permute-start.20 = (f32[4,256]{1,0:T(4,128)S(1)}, f32[4,256]{1,0:T(4,128)S(1)}, u32[]{:S(2)}, u32[]{:S(2)}) collective-permute-start(f32[4,256]{1,0:T(4,128)S(1)} %get-tuple-element.58), channel_id=1, source_target_pairs={{26,0},{28,2},{30,4},{0,6},{2,8},{4,10},{6,12},{8,14},{10,16},{12,... | collective-permute-start | bytes 12296 | tf_op jit(solution)/shard_map/ppermute | solution.py:13
  397.7 10.5 %collective-permute-start.21 = (f32[4,256]{1,0:T(4,128)S(1)}, f32[4,256]{1,0:T(4,128)S(1)}, u32[]{:S(2)}, u32[]{:S(2)}) collective-permute-start(f32[4,256]{1,0:T(4,128)S(1)} %get-tuple-element.57), channel_id=1, source_target_pairs={{2,0},{4,2},{6,4},{8,6},{10,8},{12,10},{14,12},{16,14},{18,16},{20... | collective-permute-start | bytes 12296 | tf_op jit(solution)/shard_map/ppermute | solution.py:13
  435.7 149.3 %all-reduce.17.cloned.1.call-start = ((), (), s32[]{:S(2)}) async-start(), calls=%async_computation.4 | async-start | bytes 262144 | tf_op jit(solution)/shard_map/psum | solution.py:142
  528.3 7.7 %collective-permute-start.24 = (f32[4,256]{1,0:T(4,128)S(1)}, f32[4,256]{1,0:T(4,128)S(1)}, u32[]{:S(2)}, u32[]{:S(2)}) collective-permute-start(f32[4,256]{1,0:T(4,128)S(1)} %get-tuple-element.54), channel_id=1, source_target_pairs={{30,0},{0,2},{2,4},{4,6},{6,8},{8,10},{10,12},{12,14},{14,16},{16,... | collective-permute-start | bytes 12296 | tf_op jit(solution)/shard_map/ppermute | solution.py:13
  528.4 10.6 %collective-permute-start.25 = (f32[4,256]{1,0:T(4,128)S(1)}, f32[4,256]{1,0:T(4,128)S(1)}, u32[]{:S(2)}, u32[]{:S(2)}) collective-permute-start(f32[4,256]{1,0:T(4,128)S(1)} %get-tuple-element.53), channel_id=1, source_target_pairs={{28,0},{30,2},{0,4},{2,6},{4,8},{6,10},{8,12},{10,14},{12,16},{14,... | collective-permute-start | bytes 12296 | tf_op jit(solution)/shard_map/ppermute | solution.py:13
  528.5 10.5 %collective-permute-start.26 = (f32[4,256]{1,0:T(4,128)S(1)}, f32[4,256]{1,0:T(4,128)S(1)}, u32[]{:S(2)}, u32[]{:S(2)}) collective-permute-start(f32[4,256]{1,0:T(4,128)S(1)} %get-tuple-element.52), channel_id=1, source_target_pairs={{26,0},{28,2},{30,4},{0,6},{2,8},{4,10},{6,12},{8,14},{10,16},{12,... | collective-permute-start | bytes 12296 | tf_op jit(solution)/shard_map/ppermute | solution.py:13
  528.5 10.5 %collective-permute-start.27 = (f32[4,256]{1,0:T(4,128)S(1)}, f32[4,256]{1,0:T(4,128)S(1)}, u32[]{:S(2)}, u32[]{:S(2)}) collective-permute-start(f32[4,256]{1,0:T(4,128)S(1)} %get-tuple-element.51), channel_id=1, source_target_pairs={{2,0},{4,2},{6,4},{8,6},{10,8},{12,10},{14,12},{16,14},{18,16},{20... | collective-permute-start | bytes 12296 | tf_op jit(solution)/shard_map/ppermute | solution.py:13
  (20 other events, 392.6 us)
Sparse Core Ops, SparseCore 0:
  81.3 18.0 all-reduce.8
  170.7 17.8 all-reduce.10
  300.5 18.3 all-reduce.12
  435.8 18.3 all-reduce.14
  566.6 18.3 all-reduce.16
where the time goes:
time: 640 us; the launch traced here: 639 us
  blocking collectives  171 us (27%)
  matrix products  155 us (24%)
  local copies, waits for them, and re-layouts  111 us (17%)
  waiting for transfers between devices  103 us (16%)
  starting transfers between devices  54.7 us (9%)
  between operations  24.9 us (4%)
  other arithmetic  19.9 us (3%)
    gather x30, local copies, waits for them, and re-layouts, ghosts(): jnp.take(vector_in, send_list[which], axis=1)  87.3 us
    psum x2, blocking collectives, body(): lax.psum((jnp.sum(second * middle), jnp.sum(second * second), jnp.sum(sou...  85.5 us
    psum x4, waiting for transfers between devices, apply_matrix(): return volume_rate * vector_in + lax.psum(partial_value, 'faces')  73.5 us
    ppermute x30, starting transfers between devices, passed_along(): return lax.ppermute(block, axis, route)  54.5 us
    psum x1, blocking collectives, body(): rho_now = lax.psum(jnp.sum(source_term * residual), 'cells')  42.6 us
    psum x1, blocking collectives, body(): step_alpha = rho_now / lax.psum(jnp.sum(source_term * image), 'cells')  42.6 us
    dot_general x5, matrix products, to_faces(): jnp.einsum('tfc,btc->btf', local_hot, paired, precision=highest)  34.4 us
    dot_general x5, matrix products, to_faces(): jnp.einsum('tfc,btc->btf', halo_hot, halo_windows, precision=highest)  34 us
  transfers between devices with their start and end apart: 35, of which 11 were waited for; matrix products, arithmetic and copies ran while one was open for 1% of the time, Pallas kernels for 0%

commit v1 on v0

--- a/solution.py
+++ b/solution.py
@@ -5,6 +5,11 @@
 from jax.sharding import PartitionSpec as P
 
 ITERS = 2
+
+
+def add_all(x, axis):
+    terms = lax.all_gather(x, axis)
+    return jnp.sum(terms, axis=0)
 
 
 def passed_along(block, axis, distance):
@@ -139,7 +144,7 @@
         )
         face_flux = (0.5 * central - 0.5 * wave_speed * (right_side - left_side)) * is_live
         partial_value = to_cells(face_flux, -face_flux * local_weight)
-        return volume_rate * vector_in + lax.psum(partial_value, "faces")
+        return volume_rate * vector_in + add_all(partial_value, "faces")
 
     solution_field = jnp.zeros_like(source_term)
     residual = source_term

time: 640 us -> 560 us (0.88)
  waiting for transfers between devices: 103 us -> 29.2 us
    psum x4 -> x0, waiting for transfers between devices: 73.5 us -> none  [apply_matrix(): return volume_rate * vector_in + lax.psum(partial_value, 'faces')]
    all_gather x0 -> x4, blocking collectives: none -> 7.97 us  [add_all(): terms = lax.all_gather(x, axis)]
  transfers between devices with their start and end apart: 35 -> 31, of which waited for: 11 -> 7; matrix products, arithmetic and copies ran while one was open for 1% -> 1% of each run, Pallas kernels for 0% -> 0%
where the time goes in v1:
time: 560 us; the launch traced here: 558 us
  blocking collectives  170 us (30%)
  matrix products  152 us (27%)
  local copies, waits for them, and re-layouts  111 us (20%)
  starting transfers between devices  54.5 us (10%)
  waiting for transfers between devices  29.2 us (5%)
  between operations  25.2 us (4%)
  other arithmetic  15.8 us (3%)
    gather x30, local copies, waits for them, and re-layouts, ghosts(): jnp.take(vector_in, send_list[which], axis=1)  87.3 us
    psum x2, blocking collectives, body(): lax.psum((jnp.sum(second * middle), jnp.sum(second * second), jnp.sum(sou...  81.3 us
    ppermute x30, starting transfers between devices, passed_along(): return lax.ppermute(block, axis, route)  54.5 us
    psum x1, blocking collectives, body(): step_alpha = rho_now / lax.psum(jnp.sum(source_term * image), 'cells')  40.5 us
    psum x1, blocking collectives, body(): rho_now = lax.psum(jnp.sum(source_term * residual), 'cells')  40.4 us
    dot_general x5, matrix products, to_faces(): jnp.einsum('tfc,btc->btf', local_hot, paired, precision=highest)  34.4 us
    dot_general x5, matrix products, to_faces(): jnp.einsum('tfc,btc->btf', halo_hot, halo_windows, precision=highest)  34 us
    dot_general x5, matrix products, to_faces(): left_side = jnp.einsum('tfc,btc->btf', owner_hot, blocks, precision=highest)  31.8 us
  transfers between devices with their start and end apart: 31, of which 7 were waited for; matrix products, arithmetic and copies ran while one was open for 1% of the time, Pallas kernels for 0%

profile of v1, /device:TPU:0, one launch (start us, length us, event | category | flops | bytes accessed | tf_op | source)
XLA Modules:
  0.0 558.1 jit_solution(13733861067441319154)
XLA Ops:
  42.0 6.4 %fusion.61 = f32[4,64,192]{2,0,1:T(4,128)S(1)} fusion(s32[64,192]{1,0:T(8,128)S(1)} %get-tuple-element.87, f32[4,8192]{1,0:T(4,128)S(1)} %copy-done.4), kind=kOutput, calls=%fused_computation.99 | convolution fusion | flops 77070336 | bytes 376832 | tf_op jit(solution)/shard_map/tfc,btc->btf/dot_general | solution.py:96
  54.7 6.8 %fusion.4 = f32[64,4,192]{2,1,0:T(4,128)S(1)} fusion(s32[64,192]{1,0:T(8,128)S(1)} %get-tuple-element.48, f32[64,4,256]{2,1,0:T(4,128)S(1)} %gather_fusion), kind=kOutput, calls=%fused_computation.40 | convolution fusion | flops 154140672 | bytes 507904 | tf_op jit(solution)/shard_map/tfc,btc->btf/dot_general | solution.py:98
  61.5 6.9 %fusion.56 = f32[4,64,192]{2,0,1:T(4,128)S(1)} fusion(f32[64,4,192]{2,1,0:T(4,128)S(1)} %fusion.4, s32[64,192]{1,0:T(8,128)S(1)} %get-tuple-element.47, f32[4,1,128]{2,0,1:T(4,128)S(1)} %slice.454, f32[4,63,128]{2,0,1:T(4,128)S(1)} %slice.453, f32[4,64,128]{2,0,1:T(4,128)S(1)} %bitcast.444), kind=kOutput, calls=%fused_computation.94 | convolution fusion | flops 154320896 | bytes 704512 | tf_op jit(solution)/shard_map/tfc,btc->btf/dot_general | solution.py:97
  68.8 6.9 %fusion.50 = f32[5,64,256]{2,0,1:T(8,128)S(1)} fusion(s32[64,192]{1,0:T(8,128)S(1)} %get-tuple-element.47, f32[5,64,192]{2,1,0:T(8,128)S(1)} %maximum_multiply_fusion.1), kind=kOutput, calls=%fused_computation.88 | convolution fusion | flops 191889408 | bytes 622592 | tf_op jit(solution)/shard_map/tfc,btf->btc/dot_general | solution.py:106
  81.3 18.2 %all-reduce.5.cloned.1.call-done = f32[5,8192]{1,0:T(8,128)} async-done(((f32[5,8192]{1,0:T(8,128)}), f32[5,8192]{1,0:T(8,128)}) %all-reduce.5.cloned.1.call-update) | async-done | bytes 163856 | tf_op jit(solution)/shard_map/psum | solution.py:122
  123.0 6.4 %fusion.37 = f32[64,4,192]{2,1,0:T(4,128)S(1)} fusion(s32[64,192]{1,0:T(8,128)S(1)} %get-tuple-element.87, f32[1,64,128]{2,0,1:T(1,128)S(1)} %bitcast.423, f32[3,64,128]{2,0,1:T(4,128)S(1)} %bitcast.397), kind=kOutput, calls=%fused_computation.75 | convolution fusion | flops 77103104 | bytes 376832 | tf_op jit(solution)/shard_map/tfc,btc->btf/dot_general | solution.py:96
  145.3 6.8 %fusion.3 = f32[64,4,192]{2,1,0:T(4,128)S(1)} fusion(s32[64,192]{1,0:T(8,128)S(1)} %get-tuple-element.48, f32[64,4,256]{2,1,0:T(4,128)S(1)} %gather_fusion.1), kind=kOutput, calls=%fused_computation.39 | convolution fusion | flops 154140672 | bytes 507904 | tf_op jit(solution)/shard_map/tfc,btc->btf/dot_general | solution.py:98
  152.1 6.9 %fusion.57 = f32[64,4,192]{2,1,0:T(4,128)S(1)} fusion(f32[64,4,192]{2,1,0:T(4,128)S(1)} %fusion.3, s32[64,192]{1,0:T(8,128)S(1)} %get-tuple-element.47, f32[4,1,128]{2,0,1:T(4,128)S(1)} %fusion.167, f32[4,63,128]{2,0,1:T(4,128)S(1)} %fusion.154, f32[1,64,128]{2,0,1:T(1,128)S(1)} %bitcast.425, f32[3,64,128]{2,0,1:T(4,128)S(1)} %bitcast.399), kind=kOutput, calls=%fused_computation.95 | convolution fusion | flops 154386432 | bytes 704512 | tf_op jit(solution)/shard_map/tfc,btc->btf/dot_general | solution.py:97
  172.7 40.4 %all-reduce.2 = (f32[]{:T(128)}, f32[]{:T(128)}) all-reduce(f32[]{:T(128)} %get-tuple-element.16, f32[]{:T(128)} %get-tuple-element.15), channel_id=1, replica_groups=mesh['cells'=16,'faces'=2] {'cells'}, use_global_device_ids=true, to_apply=%region_1.2 | all-reduce | flops 2 | bytes 16 | tf_op jit(solution)/shard_map/psum | solution.py:152
  235.0 6.4 %fusion.35 = f32[64,4,192]{2,1,0:T(4,128)S(1)} fusion(s32[64,192]{1,0:T(8,128)S(1)} %get-tuple-element.87, f32[1,64,128]{2,0,1:T(1,128)S(1)} %bitcast.430, f32[3,64,128]{2,0,1:T(4,128)S(1)} %bitcast.401), kind=kOutput, calls=%fused_computation.73 | convolution fusion | flops 77103104 | bytes 376832 | tf_op jit(solution)/shard_map/tfc,btc->btf/dot_general | solution.py:96
  242.8 5.6 %collective-permute-start.15 = (f32[4,256]{1,0:T(4,128)S(1)}, f32[4,256]{1,0:T(4,128)S(1)}, u32[]{:S(2)}, u32[]{:S(2)}) collective-permute-start(f32[4,256]{1,0:T(4,128)S(1)} %get-tuple-element.63), channel_id=1, source_target_pairs={{2,0},{4,2},{6,4},{8,6},{10,8},{12,10},{14,12},{16,14},{18,16},{20... | collective-permute-start | bytes 12296 | tf_op jit(solution)/shard_map/ppermute | solution.py:18
  255.6 6.8 %fusion.2 = f32[64,4,192]{2,1,0:T(4,128)S(1)} fusion(s32[64,192]{1,0:T(8,128)S(1)} %get-tuple-element.48, f32[64,4,256]{2,1,0:T(4,128)S(1)} %gather_fusion.2), kind=kOutput, calls=%fused_computation.38 | convolution fusion | flops 154140672 | bytes 507904 | tf_op jit(solution)/shard_map/tfc,btc->btf/dot_general | solution.py:98
  262.4 6.9 %fusion.58 = f32[64,4,192]{2,1,0:T(4,128)S(1)} fusion(f32[64,4,192]{2,1,0:T(4,128)S(1)} %fusion.2, s32[64,192]{1,0:T(8,128)S(1)} %get-tuple-element.47, f32[4,1,128]{2,0,1:T(4,128)S(1)} %fusion.166, f32[4,63,128]{2,0,1:T(4,128)S(1)} %fusion.153, f32[1,64,128]{2,0,1:T(1,128)S(1)} %bitcast.432, f32[3,64,128]{2,0,1:T(4,128)S(1)} %bitcast.403), kind=kOutput, calls=%fused_computation.96 | convolution fusion | flops 154386432 | bytes 704512 | tf_op jit(solution)/shard_map/tfc,btc->btf/dot_general | solution.py:97
  283.1 40.8 %all-reduce.1 = (f32[]{:T(128)}, f32[]{:T(128)}, f32[]{:T(128)}, f32[]{:T(128)}) all-reduce(f32[]{:T(128)} %get-tuple-element.14, f32[]{:T(128)} %get-tuple-element.13, f32[]{:T(128)} %get-tuple-element.12, f32[]{:T(128)} %get-tuple-element.11), channel_id=1, replica_groups=mesh['cells'=16,'faces'=2] {'cells'}, use_global_device_ids=true, to_apply=%region_19.21 | all-reduce | flops 4 | bytes 32 | tf_op jit(solution)/shard_map/psum | solution.py:160
  350.1 6.4 %fusion.33 = f32[64,4,192]{2,1,0:T(4,128)S(1)} fusion(s32[64,192]{1,0:T(8,128)S(1)} %get-tuple-element.87, f32[1,64,128]{2,0,1:T(1,128)S(1)} %bitcast.415, f32[3,64,128]{2,0,1:T(4,128)S(1)} %bitcast.393), kind=kOutput, calls=%fused_computation.71 | convolution fusion | flops 77103104 | bytes 376832 | tf_op jit(solution)/shard_map/tfc,btc->btf/dot_general | solution.py:96
  358.0 5.6 %collective-permute-start.21 = (f32[4,256]{1,0:T(4,128)S(1)}, f32[4,256]{1,0:T(4,128)S(1)}, u32[]{:S(2)}, u32[]{:S(2)}) collective-permute-start(f32[4,256]{1,0:T(4,128)S(1)} %get-tuple-element.57), channel_id=1, source_target_pairs={{2,0},{4,2},{6,4},{8,6},{10,8},{12,10},{14,12},{16,14},{18,16},{20... | collective-permute-start | bytes 12296 | tf_op jit(solution)/shard_map/ppermute | solution.py:18
  370.7 6.8 %fusion.1 = f32[64,4,192]{2,1,0:T(4,128)S(1)} fusion(s32[64,192]{1,0:T(8,128)S(1)} %get-tuple-element.48, f32[64,4,256]{2,1,0:T(4,128)S(1)} %gather_fusion.3), kind=kOutput, calls=%fused_computation.37 | convolution fusion | flops 154140672 | bytes 507904 | tf_op jit(solution)/shard_map/tfc,btc->btf/dot_general | solution.py:98
  377.5 6.9 %fusion.59 = f32[64,4,192]{2,1,0:T(4,128)S(1)} fusion(f32[64,4,192]{2,1,0:T(4,128)S(1)} %fusion.1, s32[64,192]{1,0:T(8,128)S(1)} %get-tuple-element.47, f32[4,1,128]{2,0,1:T(4,128)S(1)} %fusion.165, f32[4,63,128]{2,0,1:T(4,128)S(1)} %fusion.152, f32[1,64,128]{2,0,1:T(1,128)S(1)} %bitcast.417, f32[3,64,128]{2,0,1:T(4,128)S(1)} %bitcast.395), kind=kOutput, calls=%fused_computation.97 | convolution fusion | flops 154386432 | bytes 704512 | tf_op jit(solution)/shard_map/tfc,btc->btf/dot_general | solution.py:97
  398.0 40.5 %psum.77 = f32[]{:T(128)} all-reduce(f32[]{:T(128)} %multiply_reduce_fusion.4), channel_id=1, replica_groups=mesh['cells'=16,'faces'=2] {'cells'}, use_global_device_ids=true, to_apply=%region_26.28 | all-reduce | flops 1 | bytes 8 | tf_op jit(solution)/shard_map/psum | solution.py:156
  459.8 6.4 %fusion.31 = f32[64,4,192]{2,1,0:T(4,128)S(1)} fusion(s32[64,192]{1,0:T(8,128)S(1)} %get-tuple-element.87, f32[1,64,128]{2,0,1:T(1,128)S(1)} %bitcast.437, f32[3,64,128]{2,0,1:T(4,128)S(1)} %bitcast.405), kind=kOutput, calls=%fused_computation.69 | convolution fusion | flops 77103104 | bytes 376832 | tf_op jit(solution)/shard_map/tfc,btc->btf/dot_general | solution.py:96
  467.7 5.6 %collective-permute-start.27 = (f32[4,256]{1,0:T(4,128)S(1)}, f32[4,256]{1,0:T(4,128)S(1)}, u32[]{:S(2)}, u32[]{:S(2)}) collective-permute-start(f32[4,256]{1,0:T(4,128)S(1)} %get-tuple-element.51), channel_id=1, source_target_pairs={{2,0},{4,2},{6,4},{8,6},{10,8},{12,10},{14,12},{16,14},{18,16},{20... | collective-permute-start | bytes 12296 | tf_op jit(solution)/shard_map/ppermute | solution.py:18
  480.4 6.8 %fusion = f32[64,4,192]{2,1,0:T(4,128)S(1)} fusion(s32[64,192]{1,0:T(8,128)S(1)} %get-tuple-element.48, f32[64,4,256]{2,1,0:T(4,128)S(1)} %gather_fusion.4), kind=kOutput, calls=%fused_computation.36 | convolution fusion | flops 154140672 | bytes 507904 | tf_op jit(solution)/shard_map/tfc,btc->btf/dot_general | solution.py:98
  487.2 6.9 %fusion.60 = f32[64,4,192]{2,1,0:T(4,128)S(1)} fusion(f32[64,4,192]{2,1,0:T(4,128)S(1)} %fusion, s32[64,192]{1,0:T(8,128)S(1)} %get-tuple-element.47, f32[4,1,128]{2,0,1:T(4,128)S(1)} %fusion.164, f32[4,63,128]{2,0,1:T(4,128)S(1)} %fusion.151, f32[1,64,128]{2,0,1:T(1,128)S(1)} %bitcast.439, f32[3,64,128]{2,0,1:T(4,128)S(1)} %bitcast.407), kind=kOutput, calls=%fused_computation.98 | convolution fusion | flops 154386432 | bytes 704512 | tf_op jit(solution)/shard_map/tfc,btc->btf/dot_general | solution.py:97
  507.8 40.5 %all-reduce = (f32[]{:T(128)}, f32[]{:T(128)}) all-reduce(f32[]{:T(128)} %get-tuple-element.10, f32[]{:T(128)} %get-tuple-element.9), channel_id=1, replica_groups=mesh['cells'=16,'faces'=2] {'cells'}, use_global_device_ids=true, to_apply=%region_31.33 | all-reduce | flops 2 | bytes 16 | tf_op jit(solution)/shard_map/psum | solution.py:160
  (377 shorter events, 228.6 us)
Async XLA Ops:
  7.2 92.2 %all-reduce.5.cloned.1.call-start = ((), (), s32[]{:S(2)}) async-start(), calls=%async_computation | async-start | bytes 524288 | tf_op jit(solution)/shard_map/psum | solution.py:122
  30.6 18.8 %collective-permute-start = (f32[4,256]{1,0:T(4,128)S(1)}, f32[4,256]{1,0:T(4,128)S(1)}, u32[]{:S(2)}, u32[]{:S(2)}) collective-permute-start(f32[4,256]{1,0:T(4,128)S(1)} %get-tuple-element.78), channel_id=1, source_target_pairs={{30,0},{0,2},{2,4},{4,6},{6,8},{8,10},{10,12},{12,14},{14,16},{16,... | collective-permute-start | bytes 12296 | tf_op jit(solution)/shard_map/ppermute | solution.py:18
  33.7 17.1 %collective-permute-start.1 = (f32[4,256]{1,0:T(4,128)S(1)}, f32[4,256]{1,0:T(4,128)S(1)}, u32[]{:S(2)}, u32[]{:S(2)}) collective-permute-start(f32[4,256]{1,0:T(4,128)S(1)} %get-tuple-element.77), channel_id=1, source_target_pairs={{28,0},{30,2},{0,4},{2,6},{4,8},{6,10},{8,12},{10,14},{12,16},{14,... | collective-permute-start | bytes 12296 | tf_op jit(solution)/shard_map/ppermute | solution.py:18
  35.2 15.6 %collective-permute-start.2 = (f32[4,256]{1,0:T(4,128)S(1)}, f32[4,256]{1,0:T(4,128)S(1)}, u32[]{:S(2)}, u32[]{:S(2)}) collective-permute-start(f32[4,256]{1,0:T(4,128)S(1)} %get-tuple-element.76), channel_id=1, source_target_pairs={{26,0},{28,2},{30,4},{0,6},{2,8},{4,10},{6,12},{8,14},{10,16},{12,... | collective-permute-start | bytes 12296 | tf_op jit(solution)/shard_map/ppermute | solution.py:18
  37.6 13.2 %collective-permute-start.3 = (f32[4,256]{1,0:T(4,128)S(1)}, f32[4,256]{1,0:T(4,128)S(1)}, u32[]{:S(2)}, u32[]{:S(2)}) collective-permute-start(f32[4,256]{1,0:T(4,128)S(1)} %get-tuple-element.75), channel_id=1, source_target_pairs={{2,0},{4,2},{6,4},{8,6},{10,8},{12,10},{14,12},{16,14},{18,16},{20... | collective-permute-start | bytes 12296 | tf_op jit(solution)/shard_map/ppermute | solution.py:18
  40.9 10.0 %collective-permute-start.4 = (f32[4,256]{1,0:T(4,128)S(1)}, f32[4,256]{1,0:T(4,128)S(1)}, u32[]{:S(2)}, u32[]{:S(2)}) collective-permute-start(f32[4,256]{1,0:T(4,128)S(1)} %get-tuple-element.74), channel_id=1, source_target_pairs={{4,0},{6,2},{8,4},{10,6},{12,8},{14,10},{16,12},{18,14},{20,16},{2... | collective-permute-start | bytes 12296 | tf_op jit(solution)/shard_map/ppermute | solution.py:18
  130.6 9.5 %collective-permute-start.6 = (f32[4,256]{1,0:T(4,128)S(1)}, f32[4,256]{1,0:T(4,128)S(1)}, u32[]{:S(2)}, u32[]{:S(2)}) collective-permute-start(f32[4,256]{1,0:T(4,128)S(1)} %get-tuple-element.72), channel_id=1, source_target_pairs={{30,0},{0,2},{2,4},{4,6},{6,8},{8,10},{10,12},{12,14},{14,16},{16,... | collective-permute-start | bytes 12296 | tf_op jit(solution)/shard_map/ppermute | solution.py:18
  132.4 8.8 %collective-permute-start.7 = (f32[4,256]{1,0:T(4,128)S(1)}, f32[4,256]{1,0:T(4,128)S(1)}, u32[]{:S(2)}, u32[]{:S(2)}) collective-permute-start(f32[4,256]{1,0:T(4,128)S(1)} %get-tuple-element.71), channel_id=1, source_target_pairs={{28,0},{30,2},{0,4},{2,6},{4,8},{6,10},{8,12},{10,14},{12,16},{14,... | collective-permute-start | bytes 12296 | tf_op jit(solution)/shard_map/ppermute | solution.py:18
  133.9 7.4 %collective-permute-start.8 = (f32[4,256]{1,0:T(4,128)S(1)}, f32[4,256]{1,0:T(4,128)S(1)}, u32[]{:S(2)}, u32[]{:S(2)}) collective-permute-start(f32[4,256]{1,0:T(4,128)S(1)} %get-tuple-element.70), channel_id=1, source_target_pairs={{26,0},{28,2},{30,4},{0,6},{2,8},{4,10},{6,12},{8,14},{10,16},{12,... | collective-permute-start | bytes 12296 | tf_op jit(solution)/shard_map/ppermute | solution.py:18
  136.3 5.0 collective-permute-start.9
  242.6 7.7 %collective-permute-start.12 = (f32[4,256]{1,0:T(4,128)S(1)}, f32[4,256]{1,0:T(4,128)S(1)}, u32[]{:S(2)}, u32[]{:S(2)}) collective-permute-start(f32[4,256]{1,0:T(4,128)S(1)} %get-tuple-element.66), channel_id=1, source_target_pairs={{30,0},{0,2},{2,4},{4,6},{6,8},{8,10},{10,12},{12,14},{14,16},{16,... | collective-permute-start | bytes 12296 | tf_op jit(solution)/shard_map/ppermute | solution.py:18
  242.7 10.6 %collective-permute-start.13 = (f32[4,256]{1,0:T(4,128)S(1)}, f32[4,256]{1,0:T(4,128)S(1)}, u32[]{:S(2)}, u32[]{:S(2)}) collective-permute-start(f32[4,256]{1,0:T(4,128)S(1)} %get-tuple-element.65), channel_id=1, source_target_pairs={{28,0},{30,2},{0,4},{2,6},{4,8},{6,10},{8,12},{10,14},{12,16},{14,... | collective-permute-start | bytes 12296 | tf_op jit(solution)/shard_map/ppermute | solution.py:18
  242.8 10.5 %collective-permute-start.14 = (f32[4,256]{1,0:T(4,128)S(1)}, f32[4,256]{1,0:T(4,128)S(1)}, u32[]{:S(2)}, u32[]{:S(2)}) collective-permute-start(f32[4,256]{1,0:T(4,128)S(1)} %get-tuple-element.64), channel_id=1, source_target_pairs={{26,0},{28,2},{30,4},{0,6},{2,8},{4,10},{6,12},{8,14},{10,16},{12,... | collective-permute-start | bytes 12296 | tf_op jit(solution)/shard_map/ppermute | solution.py:18
  242.8 10.5 %collective-permute-start.15 = (f32[4,256]{1,0:T(4,128)S(1)}, f32[4,256]{1,0:T(4,128)S(1)}, u32[]{:S(2)}, u32[]{:S(2)}) collective-permute-start(f32[4,256]{1,0:T(4,128)S(1)} %get-tuple-element.63), channel_id=1, source_target_pairs={{2,0},{4,2},{6,4},{8,6},{10,8},{12,10},{14,12},{16,14},{18,16},{20... | collective-permute-start | bytes 12296 | tf_op jit(solution)/shard_map/ppermute | solution.py:18
  357.8 7.7 %collective-permute-start.18 = (f32[4,256]{1,0:T(4,128)S(1)}, f32[4,256]{1,0:T(4,128)S(1)}, u32[]{:S(2)}, u32[]{:S(2)}) collective-permute-start(f32[4,256]{1,0:T(4,128)S(1)} %get-tuple-element.60), channel_id=1, source_target_pairs={{30,0},{0,2},{2,4},{4,6},{6,8},{8,10},{10,12},{12,14},{14,16},{16,... | collective-permute-start | bytes 12296 | tf_op jit(solution)/shard_map/ppermute | solution.py:18
  357.9 10.6 %collective-permute-start.19 = (f32[4,256]{1,0:T(4,128)S(1)}, f32[4,256]{1,0:T(4,128)S(1)}, u32[]{:S(2)}, u32[]{:S(2)}) collective-permute-start(f32[4,256]{1,0:T(4,128)S(1)} %get-tuple-element.59), channel_id=1, source_target_pairs={{28,0},{30,2},{0,4},{2,6},{4,8},{6,10},{8,12},{10,14},{12,16},{14,... | collective-permute-start | bytes 12296 | tf_op jit(solution)/shard_map/ppermute | solution.py:18
  357.9 10.5 %collective-permute-start.20 = (f32[4,256]{1,0:T(4,128)S(1)}, f32[4,256]{1,0:T(4,128)S(1)}, u32[]{:S(2)}, u32[]{:S(2)}) collective-permute-start(f32[4,256]{1,0:T(4,128)S(1)} %get-tuple-element.58), channel_id=1, source_target_pairs={{26,0},{28,2},{30,4},{0,6},{2,8},{4,10},{6,12},{8,14},{10,16},{12,... | collective-permute-start | bytes 12296 | tf_op jit(solution)/shard_map/ppermute | solution.py:18
  358.0 10.5 %collective-permute-start.21 = (f32[4,256]{1,0:T(4,128)S(1)}, f32[4,256]{1,0:T(4,128)S(1)}, u32[]{:S(2)}, u32[]{:S(2)}) collective-permute-start(f32[4,256]{1,0:T(4,128)S(1)} %get-tuple-element.57), channel_id=1, source_target_pairs={{2,0},{4,2},{6,4},{8,6},{10,8},{12,10},{14,12},{16,14},{18,16},{20... | collective-permute-start | bytes 12296 | tf_op jit(solution)/shard_map/ppermute | solution.py:18
  363.6 4.9 collective-permute-start.22
  467.5 7.7 %collective-permute-start.24 = (f32[4,256]{1,0:T(4,128)S(1)}, f32[4,256]{1,0:T(4,128)S(1)}, u32[]{:S(2)}, u32[]{:S(2)}) collective-permute-start(f32[4,256]{1,0:T(4,128)S(1)} %get-tuple-element.54), channel_id=1, source_target_pairs={{30,0},{0,2},{2,4},{4,6},{6,8},{8,10},{10,12},{12,14},{14,16},{16,... | collective-permute-start | bytes 12296 | tf_op jit(solution)/shard_map/ppermute | solution.py:18
  467.6 10.6 %collective-permute-start.25 = (f32[4,256]{1,0:T(4,128)S(1)}, f32[4,256]{1,0:T(4,128)S(1)}, u32[]{:S(2)}, u32[]{:S(2)}) collective-permute-start(f32[4,256]{1,0:T(4,128)S(1)} %get-tuple-element.53), channel_id=1, source_target_pairs={{28,0},{30,2},{0,4},{2,6},{4,8},{6,10},{8,12},{10,14},{12,16},{14,... | collective-permute-start | bytes 12296 | tf_op jit(solution)/shard_map/ppermute | solution.py:18
  467.6 10.5 %collective-permute-start.26 = (f32[4,256]{1,0:T(4,128)S(1)}, f32[4,256]{1,0:T(4,128)S(1)}, u32[]{:S(2)}, u32[]{:S(2)}) collective-permute-start(f32[4,256]{1,0:T(4,128)S(1)} %get-tuple-element.52), channel_id=1, source_target_pairs={{26,0},{28,2},{30,4},{0,6},{2,8},{4,10},{6,12},{8,14},{10,16},{12,... | collective-permute-start | bytes 12296 | tf_op jit(solution)/shard_map/ppermute | solution.py:18
  467.7 10.5 %collective-permute-start.27 = (f32[4,256]{1,0:T(4,128)S(1)}, f32[4,256]{1,0:T(4,128)S(1)}, u32[]{:S(2)}, u32[]{:S(2)}) collective-permute-start(f32[4,256]{1,0:T(4,128)S(1)} %get-tuple-element.51), channel_id=1, source_target_pairs={{2,0},{4,2},{6,4},{8,6},{10,8},{12,10},{14,12},{16,14},{18,16},{20... | collective-permute-start | bytes 12296 | tf_op jit(solution)/shard_map/ppermute | solution.py:18
  473.3 4.9 collective-permute-start.28
  (16 other events, 350.9 us)
Sparse Core Ops, SparseCore 0:
  81.3 18.0 all-reduce.4
